TPU v7x, 32 devices: a whole 2x2x4 slice. The times are simulated.
32 devices in a mesh: dp: 8 (over y, x, core), mp: 4 (over z).
Axes of the slice: x: 2, y: 2, z: 4, core: 2. Of those that a mesh axis runs over, the one named last changes fastest.
Arguments:
- candidates: bfloat16 [64, 256, 768], P('dp', 'mp'), may hold values from -6 to 6
- owner_row: int32 [64], replicated, may hold values from 0 to 63, as said below
- selected: int32 [16], replicated, may hold values from 0 to 63, as said below
- dest_slot: int32 [16], replicated, may hold values from 0 to 15, as said below
- patch_weight: bfloat16 [768, 768], P(None, 'mp'), may hold values from -0.21875 to 0.21875
- positions: bfloat16 [256, 768], P(None, 'mp'), may hold values from -3 to 3
- qkv_weight: bfloat16 [768, 3, 768], P(None, None, 'mp'), may hold values from -1 to 1
- out_weight: bfloat16 [768, 768], P('mp'), may hold values from -0.21875 to 0.21875
- attn_gain: bfloat16 [768], replicated, may hold values from 0.099609375 to 1.8984375
- mlp_gain: bfloat16 [768], replicated, may hold values from 0.099609375 to 1.8984375
- up_weight: bfloat16 [768, 3072], P(None, 'mp'), may hold values from -0.21875 to 0.21875
- down_weight: bfloat16 [3072, 768], P('mp'), may hold values from -0.109375 to 0.109375
Outputs:
- layer_out: bfloat16 [16, 256, 768], P('dp', 'mp')
Inputs may be any that keep to these rules, and one draw needn't show every extreme that they name: `owner_row`: a permutation; storage row r sits on index r // 8 of dp. `selected`: distinct candidates; no index of dp stores more than 4 of them, and some index stores exactly 4. `dest_slot`: a permutation; the 2 slots s with equal s // 2 get candidates stored on different indices of dp.
All inputs are finite; a program needn't handle non-finite values.
Results may differ from a plain program's by a relative error of at most 0.012.
Values may be sent and summed in bfloat16 or wider, within the bound.
No kernel may reach another device: no remote copies, remote signals or barrier semaphores. Data moves between devices by JAX's collectives and lax.ppermute only.
A program may use at most 128 MiB of HBM per device.

v0:
```python
import jax
import jax.numpy as jnp
from jax import lax
from jax.sharding import PartitionSpec as P

PATCHES = 256
CAND_DEV = 8
SEL_DEV = 2
HEAD_DIM = 64


def norm_rows(values, gain):
    average = jnp.mean(values, axis=-1, keepdims=True)
    centred = values - average
    variance = jnp.mean(centred * centred, axis=-1, keepdims=True)
    return centred * lax.rsqrt(variance + 1e-06) * gain.astype(jnp.float32)


def local(
    candidates,
    owner_row,
    selected,
    dest_slot,
    patch_weight,
    positions,
    qkv_weight,
    out_weight,
    attn_gain,
    mlp_gain,
    up_weight,
    down_weight,
):
    learners = lax.axis_size("dp")
    own_index = lax.axis_index("dp")
    quarter = candidates.shape[1]
    pixel_width = candidates.shape[2]
    chosen_rows = jnp.take(owner_row, selected)
    slot_rows = jnp.zeros(dest_slot.shape, jnp.int32).at[dest_slot].set(chosen_rows)
    source_owner = slot_rows // CAND_DEV
    local_row = slot_rows % CAND_DEV
    stored = candidates.reshape(CAND_DEV, quarter * pixel_width)
    mine = (source_owner == own_index).reshape(learners, SEL_DEV)
    picked = jnp.sum(jnp.where(mine, local_row.reshape(learners, SEL_DEV), 0), axis=1)
    outgoing = jnp.take(stored, picked, axis=0)
    incoming = lax.all_to_all(outgoing, "dp", split_axis=0, concat_axis=0, tiled=True)
    senders = lax.dynamic_slice_in_dim(source_owner, own_index * SEL_DEV, SEL_DEV)
    arrived = jnp.take(incoming, senders, axis=0)
    own_pixels = arrived.reshape(SEL_DEV, quarter, pixel_width)
    product = jnp.einsum(
        "brp,pe->bre",
        lax.all_gather(own_pixels, "mp", axis=1, tiled=True),
        patch_weight,
        preferred_element_type=jnp.float32,
    )
    embedded = (product + positions.astype(jnp.float32)[None]).astype(jnp.bfloat16)
    activations = lax.all_gather(embedded, "mp", axis=2, tiled=True).astype(jnp.float32)
    normed = norm_rows(activations, attn_gain).astype(jnp.bfloat16)
    projected = jnp.einsum(
        "btd,dce->btce", normed, qkv_weight, preferred_element_type=jnp.float32
    ).astype(jnp.bfloat16)
    local_heads = qkv_weight.shape[2] // HEAD_DIM
    head_split = projected.reshape(SEL_DEV, PATCHES, 3, local_heads, HEAD_DIM)
    queries = head_split[:, :, 0]
    attn_keys = head_split[:, :, 1]
    attn_values = head_split[:, :, 2]
    scores = jnp.einsum(
        "bqhd,bkhd->bhqk", queries, attn_keys, preferred_element_type=jnp.float32
    ) * HEAD_DIM ** (-0.5)
    attn_probs = jax.nn.softmax(scores, axis=-1).astype(jnp.bfloat16)
    context = jnp.einsum(
        "bhqk,bkhd->bqhd", attn_probs, attn_values, preferred_element_type=jnp.float32
    ).astype(jnp.bfloat16)
    context = context.reshape(SEL_DEV, PATCHES, local_heads * HEAD_DIM)
    partial_out = jnp.einsum("bte,ed->btd", context, out_weight, preferred_element_type=jnp.float32)
    attended = lax.psum(partial_out.astype(jnp.bfloat16), "mp").astype(jnp.float32)
    after_attn = activations + attended
    normed2 = norm_rows(after_attn, mlp_gain).astype(jnp.bfloat16)
    hidden = jax.nn.gelu(
        jnp.einsum("btd,df->btf", normed2, up_weight, preferred_element_type=jnp.float32),
        approximate=False,
    ).astype(jnp.bfloat16)
    down_terms = jnp.einsum("btf,fd->btd", hidden, down_weight, preferred_element_type=jnp.float32)
    summed = lax.psum_scatter(
        down_terms.astype(jnp.bfloat16), "mp", scatter_dimension=1, tiled=True
    ).astype(jnp.float32)
    residual = lax.dynamic_slice_in_dim(after_attn, lax.axis_index("mp") * quarter, quarter, 1)
    return (residual + summed).astype(jnp.bfloat16)


def solution(mesh):
    return jax.shard_map(
        local,
        mesh=mesh,
        in_specs=(
            P("dp", "mp", None),
            P(),
            P(),
            P(),
            P(None, "mp"),
            P(None, "mp"),
            P(None, None, "mp"),
            P("mp", None),
            P(),
            P(),
            P(None, "mp"),
            P("mp", None),
        ),
        out_specs=P("dp", "mp", None),
        check_vma=False,
    )
```

profile of v0, /device:TPU:0, one launch (start us, length us, event | category | flops | bytes accessed | tf_op | source)
XLA Modules:
  0.0 183.8 jit_solution(13271876456663978697)
XLA Ops:
  6.5 0.8 compare_select_fusion.3
  7.3 1.3 gather_fusion
  8.6 0.7 compare_select_fusion.4
  9.3 0.6 scatter_custom_fusion
  10.2 1.6 copy.77
  11.8 1.1 gather_fusion.1
  13.0 0.5 broadcast.218
  13.5 1.2 reduce.4
  14.7 1.5 reshape.149
  16.2 5.2 %all-to-all-start = ((bf16[8,2,24576]{2,1,0:T(2,128)(2,1)}), bf16[8,2,24576]{2,1,0:T(2,128)(2,1)S(1)}, u32[]{:S(2)}, u32[]{:S(2)}) async-start(bf16[8,2,24576]{2,1,0:T(2,128)(2,1)} %reshape.149), calls=%async_computation | async-start | bytes 1572864 | tf_op jit(solution)/shard_map/all_to_all | solution.py:45
  21.5 0.7 convert_element_type.51
  22.3 11.7 %all-to-all-done = bf16[8,2,24576]{2,1,0:T(2,128)(2,1)S(1)} async-done(((bf16[8,2,24576]{2,1,0:T(2,128)(2,1)}), bf16[8,2,24576]{2,1,0:T(2,128)(2,1)S(1)}, u32[]{:S(2)}, u32[]{:S(2)}) %all-to-all-start) | async-done | bytes 786464 | tf_op jit(solution)/shard_map/all_to_all | solution.py:45
  34.0 0.8 reshape.150
  34.8 0.9 copy.82
  35.7 0.8 gather_fusion.2
  36.6 18.1 %all_gather.6 = bf16[2,256,768]{2,1,0:T(8,128)(2,1)S(1)} all-gather(bf16[2,64,768]{2,1,0:T(8,128)(2,1)S(1)} %bitcast_select_fusion.1), channel_id=1, replica_groups=mesh['dp'=8,'mp'=4] {'mp'}, dimensions={1}, use_global_device_ids=true | all-gather | bytes 983040 | tf_op jit(solution)/shard_map/all_gather | solution.py:51
  55.3 17.4 %all_gather.7 = bf16[2,256,768]{1,0,2:T(2,128)(2,1)S(1)} all-gather(bf16[2,256,192]{1,0,2:T(2,128)(2,1)S(1)} %copy.63), channel_id=1, replica_groups=mesh['dp'=8,'mp'=4] {'mp'}, dimensions={2}, use_global_device_ids=true | all-gather | bytes 983040 | tf_op jit(solution)/shard_map/all_gather | solution.py:56
  72.7 0.6 copy.64
  73.9 0.6 copy-done.9
  74.5 0.8 convolution_convert_fusion.2
  75.3 0.7 fusion.108
  76.0 0.9 convolution_convert_fusion.3
  76.9 1.3 convolution_convert_fusion.1
  78.5 44.0 %all-reduce.4.cloned.1.call-done = bf16[2,256,768]{2,1,0:T(8,128)(2,1)} async-done(((bf16[2,256,768]{2,1,0:T(8,128)(2,1)}), bf16[2,256,768]{2,1,0:T(8,128)(2,1)}) %all-reduce.4.cloned.1.call-update) | async-done | bytes 786448 | tf_op jit(solution)/shard_map/psum | solution.py:75
  122.5 1.5 fusion.107
  124.5 1.3 fusion.63
  125.7 4.4 %convolution_convert_fusion = bf16[2,256,768]{2,1,0:T(8,128)(2,1)S(1)} fusion(bf16[768,768]{1,0:T(8,128)(2,1)S(1)} %copy-done.8, f32[2,256,768]{2,1,0:T(8,128)S(1)} %get-tuple-element.13, u8[256,768]{1,0:T(8,128)(4,1)S(1)} %get-tuple-element.6, u8[256,768]{1,0:T(8,128)(4,1)S(1)} %get-tuple-element.5), kind=kOutput, calls=%fused_computation.41 | convolution fusion | flops 631898112 | bytes 3932160 | tf_op jit(solution)/shard_map/btf,fd->btd/dot_general | solution.py:82
  130.2 1.7 copy.69
  131.9 0.6 dynamic-slice
  133.2 42.0 %all-reduce.6.cloned.1.call-done = bf16[2,256,768]{2,0,1:T(2,128)(2,1)} async-done(((bf16[2,256,768]{2,0,1:T(2,128)(2,1)}), bf16[2,256,768]{2,0,1:T(2,128)(2,1)}) %all-reduce.6.cloned.1.call-update) | async-done | bytes 786448
  175.2 1.1 constant_dynamic-slice_fusion
  176.3 0.7 add_convert_fusion
  (47 shorter events, 2.6 us)
Async XLA Ops:
  6.5 117.9 %copy-start = (bf16[768,768]{1,0:T(8,128)(2,1)S(1)}, bf16[768,768]{1,0:T(8,128)(2,1)}, u32[]{:S(2)}) copy-start(bf16[768,768]{1,0:T(8,128)(2,1)} %param.22) | copy-start | bytes 3538948
  14.7 6.8 %copy-start.5 = (bf16[256,192]{0,1:T(8,128)(2,1)S(1)}, bf16[256,192]{0,1:T(8,128)(2,1)}, u32[]{:S(2)}) copy-start(bf16[256,192]{0,1:T(8,128)(2,1)} %param.17) | copy-start | bytes 294916
  14.7 7.5 %copy-start.6 = (bf16[768]{0:T(1024)(128)(2,1)S(1)}, bf16[768]{0:T(1024)(128)(2,1)}, u32[]{:S(2)}) copy-start(bf16[768]{0:T(1024)(128)(2,1)} %param.20) | copy-start | bytes 4612
  16.2 17.8 %all-to-all-start = ((bf16[8,2,24576]{2,1,0:T(2,128)(2,1)}), bf16[8,2,24576]{2,1,0:T(2,128)(2,1)S(1)}, u32[]{:S(2)}, u32[]{:S(2)}) async-start(bf16[8,2,24576]{2,1,0:T(2,128)(2,1)} %reshape.149), calls=%async_computation | async-start | bytes 1572864 | tf_op jit(solution)/shard_map/all_to_all | solution.py:45
  21.4 101.1 %all-reduce.4.cloned.1.call-start = ((), (), s32[]{:S(2)}) async-start(), calls=%async_computation.1 | async-start | bytes 1572864 | tf_op jit(solution)/shard_map/psum | solution.py:75
  35.7 19.0 %copy-start.2 = (f32[256,192]{0,1:T(8,128)S(1)}, f32[256,192]{0,1:T(8,128)}, u32[]{:S(2)}) copy-start(f32[256,192]{0,1:T(8,128)} %convert_element_type.51) | copy-start | bytes 589828
  35.7 19.0 %copy-start.4 = (bf16[768,192]{0,1:T(8,128)(2,1)S(1)}, bf16[768,192]{0,1:T(8,128)(2,1)}, u32[]{:S(2)}) copy-start(bf16[768,192]{0,1:T(8,128)(2,1)} %param.16) | copy-start | bytes 884740
  73.3 1.2 copy-start.9
  76.0 1.0 copy-start.3
  76.9 1.6 copy-start.7
  78.3 96.9 %all-reduce.6.cloned.1.call-start = ((), (), s32[]{:S(2)}) async-start(), calls=%async_computation.2 | async-start | bytes 1572864
  122.5 1.5 copy-start.1
  124.4 1.3 copy-start.8
  130.2 1.8 copy-start.10
Sparse Core Ops, SparseCore 0:
  78.4 44.0 all-reduce.3
  132.0 43.1 all-reduce.5
where the time goes:
time: 184 us
  waiting for transfers between devices  97.8 us (53%)
  blocking collectives  35.5 us (19%)
  between operations  14.3 us (8%)
  local copies, waits for them, and re-layouts  14 us (8%)
  matrix products  9.79 us (5%)
  other arithmetic  7.02 us (4%)
  starting transfers between devices  5.46 us (3%)
    psum x1, waiting for transfers between devices, local(): lax.psum(partial_out.astype(jnp.bfloat16), 'mp').astype(jnp.float32)  44 us
    unnamed x3, waiting for transfers between devices  42.1 us
    all_gather x1, blocking collectives, local(): lax.all_gather(own_pixels, 'mp', axis=1, tiled=True)  18.1 us
    all_gather x1, blocking collectives, local(): lax.all_gather(embedded, 'mp', axis=2, tiled=True).astype(jnp.float32)  17.4 us
    all_to_all x1, waiting for transfers between devices, local(): lax.all_to_all(outgoing, 'dp', split_axis=0, concat_axis=0, tiled=True)  11.7 us
    unnamed x28, local copies, waits for them, and re-layouts  7.11 us
    all_to_all x1, starting transfers between devices, local(): lax.all_to_all(outgoing, 'dp', split_axis=0, concat_axis=0, tiled=True)  5.2 us
    dot_general x1, matrix products, local(): jnp.einsum('btf,fd->btd', hidden, down_weight, preferred_element_type=jnp...  4.43 us
  transfers between devices with their start and end apart: 3, of which 3 were waited for; matrix products, arithmetic and copies ran while one was open for 1% of the time, Pallas kernels for 0%

commit v1 on v0

--- a/solution.py
+++ b/solution.py
@@ -53,7 +53,7 @@
         preferred_element_type=jnp.float32,
     )
     embedded = (product + positions.astype(jnp.float32)[None]).astype(jnp.bfloat16)
-    activations = lax.all_gather(embedded, "mp", axis=2, tiled=True).astype(jnp.float32)
+    activations = jnp.concatenate(jax.lax.all_gather(embedded, "mp"), axis=2).astype(jnp.float32)
     normed = norm_rows(activations, attn_gain).astype(jnp.bfloat16)
     projected = jnp.einsum(
         "btd,dce->btce", normed, qkv_weight, preferred_element_type=jnp.float32

time: 184 us -> 165 us (0.90)
  waiting for transfers between devices: 97.8 us -> 76.6 us
  matrix products: 9.79 us -> 13.2 us
  local copies, waits for them, and re-layouts: 14 us -> 12.1 us
    unnamed x3 -> x2, waiting for transfers between devices: 42.1 us -> 0.03 us
    reduce_scatter x0 -> x1, waiting for transfers between devices: none -> 22.6 us  [local(): lax.psum_scatter(down_terms.astype(jnp.bfloat16), 'mp', scatter_dimension...]
    unnamed x28 -> x22, local copies, waits for them, and re-layouts: 7.11 us -> 5.99 us
where the time goes in v1:
time: 165 us
  waiting for transfers between devices  76.6 us (46%)
  blocking collectives  35.6 us (22%)
  between operations  13.7 us (8%)
  matrix products  13.2 us (8%)
  local copies, waits for them, and re-layouts  12.1 us (7%)
  other arithmetic  8.16 us (5%)
  starting transfers between devices  5.28 us (3%)
    psum x1, waiting for transfers between devices, local(): lax.psum(partial_out.astype(jnp.bfloat16), 'mp').astype(jnp.float32)  42.3 us
    reduce_scatter x1, waiting for transfers between devices, local(): lax.psum_scatter(down_terms.astype(jnp.bfloat16), 'mp', scatter_dimension...  22.6 us
    all_gather x1, blocking collectives, local(): lax.all_gather(own_pixels, 'mp', axis=1, tiled=True)  18.1 us
    all_gather x1, blocking collectives, local(): jax.lax.all_gather(embedded, 'mp')  17.6 us
    all_to_all x1, waiting for transfers between devices, local(): lax.all_to_all(outgoing, 'dp', split_axis=0, concat_axis=0, tiled=True)  11.7 us
    unnamed x22, local copies, waits for them, and re-layouts  5.99 us
    all_to_all x1, starting transfers between devices, local(): lax.all_to_all(outgoing, 'dp', split_axis=0, concat_axis=0, tiled=True)  5.2 us
    dot_general x1, matrix products, local(): jnp.einsum('btf,fd->btd', hidden, down_weight, preferred_element_type=jnp...  5.16 us
  transfers between devices with their start and end apart: 3, of which 3 were waited for; matrix products, arithmetic and copies ran while one was open for 1% of the time, Pallas kernels for 0%

profile of v1, /device:TPU:0, one launch (start us, length us, event | category | flops | bytes accessed | tf_op | source)
XLA Modules:
  0.0 164.7 jit_solution(15594938857447014045)
XLA Ops:
  6.5 0.8 compare_select_fusion.3
  7.3 1.3 gather_fusion
  8.6 0.7 compare_select_fusion.4
  9.3 0.6 scatter_custom_fusion
  10.2 1.6 copy.48
  11.8 1.1 gather_fusion.1
  13.0 0.5 broadcast.219
  13.5 1.2 reduce.6
  14.7 1.5 reshape.156
  16.2 5.2 %all-to-all-start = ((bf16[8,2,24576]{2,1,0:T(2,128)(2,1)}), bf16[8,2,24576]{2,1,0:T(2,128)(2,1)S(1)}, u32[]{:S(2)}, u32[]{:S(2)}) async-start(bf16[8,2,24576]{2,1,0:T(2,128)(2,1)} %reshape.156), calls=%async_computation | async-start | bytes 1572864 | tf_op jit(solution)/shard_map/all_to_all | solution.py:45
  21.5 0.7 convert_element_type.62
  22.3 11.7 %all-to-all-done = bf16[8,2,24576]{2,1,0:T(2,128)(2,1)S(1)} async-done(((bf16[8,2,24576]{2,1,0:T(2,128)(2,1)}), bf16[8,2,24576]{2,1,0:T(2,128)(2,1)S(1)}, u32[]{:S(2)}, u32[]{:S(2)}) %all-to-all-start) | async-done | bytes 786464 | tf_op jit(solution)/shard_map/all_to_all | solution.py:45
  34.0 0.8 reshape.157
  34.8 0.9 copy.52
  35.7 0.8 gather_fusion.2
  36.6 18.1 %all_gather.9 = bf16[2,256,768]{2,1,0:T(8,128)(2,1)S(1)} all-gather(bf16[2,64,768]{2,1,0:T(8,128)(2,1)S(1)} %bitcast_select_fusion.1), channel_id=1, replica_groups=mesh['dp'=8,'mp'=4] {'mp'}, dimensions={1}, use_global_device_ids=true | all-gather | bytes 983040 | tf_op jit(solution)/shard_map/all_gather | solution.py:51
  54.7 0.4 fusion.15
  55.1 17.6 %all-gather = bf16[8,256,192]{1,2,0:T(8,128)(2,1)S(1)} all-gather(bf16[2,256,192]{1,2,0:T(8,128)(2,1)S(1)} %fusion.15), channel_id=2, replica_groups=mesh['dp'=8,'mp'=4] {'mp'}, dimensions={0}, use_global_device_ids=true | all-gather | bytes 983040 | tf_op jit(solution)/shard_map/all_gather | solution.py:56
  73.0 0.2 multiply_reduce_fusion.1
  73.3 1.0 copy-done.8
  74.4 1.5 convolution_convert_fusion.2
  75.9 1.7 %fusion.104 = f32[2,3,256]{2,1,0:T(4,128)S(1)} fusion(bf16[2,256,3,3,64]{1,4,3,2,0:T(8,128)(2,1)} %bitcast.10), kind=kOutput, calls=%fused_computation.159 | convolution fusion | flops 51511552 | bytes 399360 | tf_op jit(solution)/shard_map/sub | solution.py:69
  77.6 2.0 %convolution_convert_fusion.3 = bf16[2,3,64,256]{3,2,1,0:T(8,128)(2,1)S(1)} fusion(f32[2,3,256]{2,1,0:T(4,128)S(1)} %fusion.104, bf16[2,256,3,3,64]{1,4,3,2,0:T(8,128)(2,1)} %bitcast.10), kind=kOutput, calls=%fused_computation.45 | convolution fusion | flops 102336256 | bytes 792576 | tf_op jit(solution)/shard_map/bhqk,bkhd->bqhd/dot_general | solution.py:70
  79.7 1.3 convolution_convert_fusion.1
  81.1 1.6 copy.39
  82.7 42.3 %all-reduce.2.cloned.1.call-done = bf16[2,256,768]{2,1,0:T(8,128)(2,1)} async-done(((bf16[2,256,768]{2,1,0:T(8,128)(2,1)}), bf16[2,256,768]{2,1,0:T(8,128)(2,1)}) %all-reduce.2.cloned.1.call-update) | async-done | bytes 786448 | tf_op jit(solution)/shard_map/psum | solution.py:75
  125.0 1.8 %fusion.103 = (f32[2,256]{1,0:T(2,128)S(1)}, f32[2,256,768]{2,1,0:T(8,128)S(1)}) fusion(f32[2,256,768]{2,1,0:T(8,128)} %copy.39, bf16[2,256,768]{2,1,0:T(8,128)(2,1)} %all-reduce.2.cloned.1.call-done), kind=kLoop, calls=%fused_computation.158 | loop fusion | flops 1179136 | bytes 3934208 | tf_op jit(solution)/shard_map/reduce_sum | solution.py:13
  126.9 0.3 multiply_reduce_fusion
  127.2 1.1 fusion.59
  128.5 5.2 %convolution_convert_fusion = bf16[2,256,768]{2,1,0:T(8,128)(2,1)} fusion(bf16[768,768]{1,0:T(8,128)(2,1)S(1)} %copy-done.7, f32[2,256,768]{2,1,0:T(8,128)S(1)} %get-tuple-element.13, u8[256,768]{1,0:T(8,128)(4,1)S(1)} %get-tuple-element.6, u8[256,768]{1,0:T(8,128)(4,1)S(1)} %get-tuple-element.5), kind=kOutput, calls=%fused_computation.37 | convolution fusion | flops 631898112 | bytes 3932160 | tf_op jit(solution)/shard_map/btf,fd->btd/dot_general | solution.py:82
  133.7 22.6 %reduce-scatter.2.cloned.1.call-done = bf16[2,64,768]{2,1,0:T(8,128)(2,1)} async-done(((bf16[2,256,768]{2,1,0:T(8,128)(2,1)}), bf16[2,64,768]{2,1,0:T(8,128)(2,1)}) %reduce-scatter.2.cloned.1.call-update) | async-done | bytes 196624 | tf_op jit(solution)/shard_map/reduce_scatter | solution.py:83
  156.2 1.6 add_convert_fusion
  (41 shorter events, 1.3 us)
Async XLA Ops:
  6.5 120.7 %copy-start = (bf16[768,768]{1,0:T(8,128)(2,1)S(1)}, bf16[768,768]{1,0:T(8,128)(2,1)}, u32[]{:S(2)}) copy-start(bf16[768,768]{1,0:T(8,128)(2,1)} %param.22) | copy-start | bytes 3538948
  14.7 6.8 %copy-start.5 = (bf16[768]{0:T(1024)(128)(2,1)S(1)}, bf16[768]{0:T(1024)(128)(2,1)}, u32[]{:S(2)}) copy-start(bf16[768]{0:T(1024)(128)(2,1)} %param.20) | copy-start | bytes 4612
  14.7 6.8 %copy-start.4 = (bf16[256,192]{0,1:T(8,128)(2,1)S(1)}, bf16[256,192]{0,1:T(8,128)(2,1)}, u32[]{:S(2)}) copy-start(bf16[256,192]{0,1:T(8,128)(2,1)} %param.17) | copy-start | bytes 294916
  16.2 17.8 %all-to-all-start = ((bf16[8,2,24576]{2,1,0:T(2,128)(2,1)}), bf16[8,2,24576]{2,1,0:T(2,128)(2,1)S(1)}, u32[]{:S(2)}, u32[]{:S(2)}) async-start(bf16[8,2,24576]{2,1,0:T(2,128)(2,1)} %reshape.156), calls=%async_computation | async-start | bytes 1572864 | tf_op jit(solution)/shard_map/all_to_all | solution.py:45
  21.4 103.6 %all-reduce.2.cloned.1.call-start = ((), (), s32[]{:S(2)}) async-start(), calls=%async_computation.2 | async-start | bytes 1572864 | tf_op jit(solution)/shard_map/psum | solution.py:75
  35.7 19.0 %copy-start.1 = (f32[256,192]{0,1:T(8,128)S(1)}, f32[256,192]{0,1:T(8,128)}, u32[]{:S(2)}) copy-start(f32[256,192]{0,1:T(8,128)} %convert_element_type.62) | copy-start | bytes 589828
  35.7 19.0 %copy-start.3 = (bf16[768,192]{0,1:T(8,128)(2,1)S(1)}, bf16[768,192]{0,1:T(8,128)(2,1)}, u32[]{:S(2)}) copy-start(bf16[768,192]{0,1:T(8,128)(2,1)} %param.16) | copy-start | bytes 884740
  73.2 1.2 copy-start.8
  77.6 2.1 %copy-start.2 = (bf16[192,768]{1,0:T(8,128)(2,1)S(1)}, bf16[192,768]{1,0:T(8,128)(2,1)}, u32[]{:S(2)}) copy-start(bf16[192,768]{1,0:T(8,128)(2,1)} %param.19) | copy-start | bytes 884740
  79.6 1.4 copy-start.6
  81.0 75.2 %reduce-scatter.2.cloned.1.call-start = ((), (), s32[]{:S(2)}) async-start(), calls=%async_computation.3 | async-start | bytes 983040 | tf_op jit(solution)/shard_map/reduce_scatter | solution.py:83
  127.2 1.3 copy-start.7
Sparse Core Ops, SparseCore 0:
  81.1 43.8 all-reduce.1
  133.8 22.3 reduce-scatter.1
